TPU v7x, 32 devices: a whole 2x2x4 slice. The times are simulated.
32 devices in a mesh: occ: 4 (over y, core), vir: 8 (over z, x).
Axes of the slice: x: 2, y: 2, z: 4, core: 2. Of those that a mesh axis runs over, the one named last changes fastest.
Arguments:
- amplitudes: bfloat16 [2048, 4096], P('occ', 'vir'), may hold values from -6 to 6
- hole_integrals: bfloat16 [2048, 2048], P('occ'), may hold values from -0.375 to 0.375
- particle_integrals: bfloat16 [4096, 4096], P('vir'), may hold values from -0.375 to 0.375
- occ_irrep: int32 [32], replicated, may hold values from 0 to 7
- vir_irrep: int32 [64], replicated, may hold values from 0 to 7
- occ_energy: float32 [2048], P('occ'), may hold values from -1.5 to -0.5
- vir_energy: float32 [4096], P('vir'), may hold values from 0.5 to 2.5
Outputs:
- update: float32 [4096, 2048], P('vir', 'occ')
All inputs are finite; a program needn't handle non-finite values.
Results may differ from a plain program's by a relative error of at most 0.0003.
Values may be sent and summed in bfloat16 or wider, within the bound.
A program may use at most 128 MiB of HBM per device.

v0:
```python
import jax
import jax.numpy as jnp
from jax import lax
from jax.sharding import PartitionSpec as P

TILE = 64


def per_device(
    amplitudes, hole_integrals, particle_integrals, occ_irrep, vir_irrep, occ_energy, vir_energy
):
    own_rows = amplitudes.shape[0]
    own_pairs = amplitudes.shape[1]
    zero_value = jnp.zeros((), jnp.bfloat16)
    occ_labels = jnp.repeat(occ_irrep, TILE)
    vir_labels = jnp.repeat(vir_irrep, TILE)
    own_occ = lax.dynamic_slice_in_dim(occ_labels, lax.axis_index("occ") * own_rows, own_rows)
    own_vir = lax.dynamic_slice_in_dim(vir_labels, lax.axis_index("vir") * own_pairs, own_pairs)
    hole_masked = jnp.where(own_occ[:, None] == occ_labels[None, :], hole_integrals, zero_value)
    contract_first = (((0,), (1,)), ((), ()))
    hole = lax.dot_general(
        lax.all_gather(amplitudes, "occ", axis=0, tiled=True),
        hole_masked,
        contract_first,
        preferred_element_type=jnp.float32,
    )
    slab_masked = jnp.where(own_vir[:, None] == vir_labels[None, :], particle_integrals, zero_value)
    particle = lax.psum_scatter(
        lax.dot_general(
            slab_masked, amplitudes, contract_first, preferred_element_type=jnp.float32
        ),
        "vir",
        scatter_dimension=0,
        tiled=True,
    )
    energy_gap = vir_energy[:, None] - occ_energy[None, :]
    return (hole + particle) / energy_gap


def solution(mesh):
    placed = (P("occ", "vir"), P("occ", None), P("vir", None), P(), P(), P("occ"), P("vir"))
    return jax.shard_map(
        per_device, mesh=mesh, in_specs=placed, out_specs=P("vir", "occ"), check_vma=False
    )
```

profile of v0, /device:TPU:0, one launch (start us, length us, event | category | flops | bytes accessed | tf_op | source)
XLA Modules:
  0.0 179.7 jit_solution(1815202672080562376)
XLA Ops:
  7.4 0.0 all-gather.2.cloned.1.call-start
  7.4 0.7 all-gather.2.cloned.1.call-update
  8.1 0.0 reduce-scatter.2.cloned.1.call-start
  8.1 0.7 broadcast_in_dim.20
  8.9 0.1 reshape.13
  8.9 0.1 dynamic_slice.7
  9.0 8.1 %fusion = f32[4096,512]{0,1:T(8,128)} fusion(bf16[512,512]{1,0:T(8,128)(2,1)} %param.7, bf16[512,4096]{1,0:T(8,128)(2,1)} %param.9, s32[4096]{0:T(1024)S(1)} %reshape.13, s32[512]{0:T(512)S(1)} %dynamic_slice.7), kind=kOutput, calls=%fused_computation.1 | convolution fusion | flops 2151677952 | bytes 13125632 | tf_op jit(solution)/shard_map/dot_general | solution.py:29
  17.1 0.0 copy-start
  17.1 0.0 copy-start.1
  17.1 0.0 copy-start.2
  17.1 0.0 copy-start.3
  17.1 0.0 reduce-scatter.2.cloned.1.call-update
  17.1 0.6 copy-done
  17.8 0.1 broadcast_in_dim.18
  17.8 0.1 reshape.12
  17.9 0.1 dynamic_slice.6
  18.0 17.1 %all-gather.2.cloned.1.call-done = bf16[2048,512]{1,0:T(8,128)(2,1)} async-done(((bf16[512,512]{1,0:T(8,128)(2,1)}), bf16[2048,512]{1,0:T(8,128)(2,1)}) %all-gather.2.cloned.1.call-update) | async-done | bytes 2097168 | tf_op jit(solution)/shard_map/all_gather | solution.py:22
  35.0 132.7 %reduce-scatter.2.cloned.1.call-done = f32[512,512]{0,1:T(8,128)} async-done(((f32[4096,512]{0,1:T(8,128)}), f32[512,512]{0,1:T(8,128)}) %reduce-scatter.2.cloned.1.call-update) | async-done | bytes 1048592 | tf_op jit(solution)/shard_map/reduce_scatter | solution.py:28
  167.8 0.0 copy-done.1
  167.8 0.0 copy-done.2
  167.8 0.0 copy-done.3
  167.8 3.2 %subtract_divide_fusion = f32[512,512]{0,1:T(8,128)S(1)} fusion(f32[512,512]{0,1:T(8,128)} %reduce-scatter.2.cloned.1.call-done, bf16[2048,512]{1,0:T(8,128)(2,1)} %all-gather.2.cloned.1.call-done, bf16[512,2048]{1,0:T(8,128)(2,1)S(1)} %copy-done.1, s32[2048]{0:T(1024)S(1)} %reshape.12, s32[512]{0:T(512)S(1)} %dynamic_slice.6, f32[512]{0:T(512)S(1)} %copy-done.2, ...), kind=kOutput, calls=%fused_computation.11 | convolution fusion | flops 1076625408 | bytes 6305792 | tf_op jit(solution)/shard_map/dot_general | solution.py:21
  171.0 1.3 copy.9
Async XLA Ops:
  7.4 27.7 %all-gather.2.cloned.1.call-start = ((), (), s32[]{:S(2)}) async-start(), calls=%async_computation.1 | async-start | bytes 2621440 | tf_op jit(solution)/shard_map/all_gather | solution.py:22
  8.1 159.7 %reduce-scatter.2.cloned.1.call-start = ((), (), s32[]{:S(2)}) async-start(), calls=%async_computation.2 | async-start | bytes 9437184 | tf_op jit(solution)/shard_map/reduce_scatter | solution.py:28
  17.1 0.7 copy-start
  17.1 150.7 %copy-start.1 = (bf16[512,2048]{1,0:T(8,128)(2,1)S(1)}, bf16[512,2048]{1,0:T(8,128)(2,1)}, u32[]{:S(2)}) copy-start(bf16[512,2048]{1,0:T(8,128)(2,1)} %param.8) | copy-start | bytes 6291460
  17.1 150.7 %copy-start.2 = (f32[512]{0:T(512)S(1)}, f32[512]{0:T(512)}, u32[]{:S(2)}) copy-start(f32[512]{0:T(512)} %param.12) | copy-start | bytes 6148
  17.1 150.7 %copy-start.3 = (f32[512]{0:T(512)S(1)}, f32[512]{0:T(512)}, u32[]{:S(2)}) copy-start(f32[512]{0:T(512)} %param.13) | copy-start | bytes 6148
Sparse Core Ops, SparseCore 0:
  9.7 25.2 all-gather.1
Sparse Core Ops, SparseCore 1:
  17.2 150.5 reduce-scatter.1
where the time goes:
time: 180 us
  waiting for transfers between devices  151 us (84%)
  between operations  14.9 us (8%)
  matrix products  11.2 us (6%)
  local copies, waits for them, and re-layouts  3.02 us (2%)
    reduce_scatter x1, waiting for transfers between devices, per_device(): lax.psum_scatter(lax.dot_general(slab_masked, amplitudes, contract_first,...  133 us
    all_gather x1, waiting for transfers between devices, per_device(): lax.all_gather(amplitudes, 'occ', axis=0, tiled=True)  17.1 us
    dot_general x1, matrix products, per_device(): lax.dot_general(slab_masked, amplitudes, contract_first, preferred_elemen...  8.08 us
  transfers between devices with their start and end apart: 2, of which 2 were waited for; matrix products, arithmetic and copies ran while one was open for 5% of the time, Pallas kernels for 0%

commit v1 on v0

v1 whole, which is shorter than its diff:
```python
import functools

import jax
import jax.numpy as jnp
from jax import lax
from jax.experimental import pallas as pl
from jax.experimental.pallas import tpu as pltpu
from jax.sharding import PartitionSpec as P

TILE = 64
CORES = 2
CHUNKS = 4
MESH = pl.DeviceIdType.MESH


def kernel(
    lines, width, groups, amp, hole, slab, occ_irrep, vir_irrep, occ_labels, vir_labels, occ_e, vir_e, out,
    slab_all, slab_masked, rows_all, cols_all, hole_masked, mine, theirs, acc,
    send_sem, slab_sem, rows_sem, cols_sem, part_sem, local_sem,
):
    p_own, q_own = amp.shape
    o, v = lax.axis_index("occ"), lax.axis_index("vir")
    h, c = o // CORES, lax.rem(o, CORES)
    z, x = v // width, lax.rem(v, width)
    occ_size = groups * CORES
    share = q_own // occ_size
    step_rows = p_own // CHUNKS
    partner = h * CORES + (1 - c)
    sent = []

    def shift(i, d, n):
        return lax.rem(i + d, n)

    others_h = [shift(h, d, groups) for d in range(1, groups)]
    others_z = [shift(z, d, lines) for d in range(1, lines)]
    others_x = [shift(x, d, width) for d in range(1, width)]

    def send(src, dst, recv, device, when=None):
        copy = pltpu.make_async_remote_copy(
            src_ref=src, dst_ref=dst, send_sem=send_sem.at[len(sent)], recv_sem=recv,
            device_id=device, device_id_type=MESH,
        )
        sent.append((copy, when))
        if when is None:
            copy.start()
        else:
            pl.when(when)(copy.start)

    def landed(ref, sem):
        pltpu.make_async_copy(ref, ref, sem).wait()

    barrier = pltpu.get_barrier_semaphore()
    peers = [(partner, v)] + [(g * CORES + c, v) for g in others_h]
    peers += [(o, g * width + x) for g in others_z] + [(o, z * width + g) for g in others_x]
    for peer in peers:
        pl.semaphore_signal(barrier, inc=1, device_id=peer, device_id_type=MESH)
    pl.semaphore_wait(barrier, len(peers))

    own_cols = pltpu.make_async_copy(
        slab.at[:, pl.ds(pl.multiple_of(z * width * q_own, q_own), width * q_own)],
        slab_all.at[pl.ds(pl.multiple_of(z * q_own, q_own), q_own), :],
        local_sem.at[0],
    )
    own_cols.start()
    own_rows = pltpu.make_async_copy(amp, rows_all.at[:, pl.ds(pl.multiple_of(z * q_own, q_own), q_own)], local_sem.at[1])
    own_rows.start()
    own_pairs = pltpu.make_async_copy(amp, cols_all.at[pl.ds(pl.multiple_of(o * p_own, p_own), p_own), :], local_sem.at[2])
    own_pairs.start()

    def slab_piece(zz, oo, xx):
        return slab_all.at[
            pl.ds(pl.multiple_of(zz * q_own + oo * share, share), share),
            pl.ds(pl.multiple_of(xx * q_own, q_own), q_own),
        ]

    def slab_send(xx):
        for zz in others_z:
            send(
                slab.at[
                    pl.ds(pl.multiple_of(o * share, share), share),
                    pl.ds(pl.multiple_of((zz * width + xx) * q_own, q_own), q_own),
                ],
                slab_piece(z, o, xx), slab_sem.at[z, o, xx], (o, zz * width + x),
            )

    def slab_share(xx):
        for zz in reversed(others_z):
            piece, sem = slab_piece(zz, o, xx), slab_sem.at[zz, o, xx]
            landed(piece, sem)
            for g in others_h:
                send(piece, piece, sem, (g * CORES + c, v))
            send(piece, piece, sem, (partner, v))

    def slab_pass(xx):
        for zz in reversed(others_z):
            for g in others_h:
                piece, sem = slab_piece(zz, g * CORES + c, xx), slab_sem.at[zz, g * CORES + c, xx]
                landed(piece, sem)
                send(piece, piece, sem, (partner, v))

    def slab_mask(xx):
        for zz in others_z:
            for g in range(groups):
                landed(slab_piece(zz, g * CORES + 1 - c, xx), slab_sem.at[zz, g * CORES + 1 - c, xx])
        tiles = q_own // TILE
        columns = pl.ds(pl.multiple_of(xx * q_own, q_own), q_own)
        labels = vir_labels[:, pl.ds(pl.multiple_of((z * width + xx) * q_own, q_own), q_own)]

        @pl.loop(0, lines * tiles)
        def _(i):
            label = vir_irrep[((i // tiles) * width + x) * tiles + lax.rem(i, tiles)]
            at = pl.ds(pl.multiple_of(i * TILE, TILE), TILE)
            block = slab_all[at, columns].astype(jnp.float32)
            slab_masked[at, columns] = jnp.where(labels == label, block, 0.0).astype(jnp.bfloat16)

    def rows_piece(zz, k):
        return rows_all.at[pl.ds(k * step_rows, step_rows), pl.ds(pl.multiple_of(zz * q_own, q_own), q_own)]

    up, down = (o, (z + 1) * width + x), (o, (z - 1) * width + x)
    has_up, has_down = z < lines - 1, z > 0

    def rows_send(k):
        src = amp.at[pl.ds(k * step_rows, step_rows), :]
        send(src, rows_piece(z, k), rows_sem.at[z, k], up, has_up)
        send(src, rows_piece(z, k), rows_sem.at[z, k], down, has_down)

    def rows_relay(k):
        for d in range(1, lines):
            for zz, there, onward, device in (
                (z - d, z - d >= 0, has_up, up), (z + d, z + d < lines, has_down, down),
            ):
                piece, sem = rows_piece(zz, k), rows_sem.at[lax.rem(zz + lines, lines), k]
                pl.when(there)(functools.partial(landed, piece, sem))
                if d < lines - 1:
                    send(piece, piece, sem, device, jnp.logical_and(there, onward))

    def pairs_piece(oo):
        return cols_all.at[pl.ds(pl.multiple_of(oo * p_own, p_own), p_own), :]

    for xx in others_x:
        slab_send(xx)
    for k in range(CHUNKS):
        rows_send(k)
    for g in others_h:
        send(amp, pairs_piece(o), cols_sem.at[o], (g * CORES + c, v))
    send(amp, pairs_piece(o), cols_sem.at[o], (partner, v))

    tiles = p_own // TILE

    @pl.loop(0, tiles)
    def _(i):
        at = pl.ds(pl.multiple_of(i * TILE, TILE), TILE)
        label = occ_irrep[o * tiles + i]
        hole_masked[at, :] = jnp.where(
            occ_labels[...] == label, hole[at, :].astype(jnp.float32), 0.0
        ).astype(jnp.bfloat16)

    for xx in others_x:
        slab_share(xx)
    rows_relay(0)
    for xx in others_x:
        slab_pass(xx)
    for k in range(1, CHUNKS):
        rows_relay(k)
    slab_send(x)
    for g in others_h:
        landed(pairs_piece(g * CORES + c), cols_sem.at[g * CORES + c])
        send(pairs_piece(g * CORES + c), pairs_piece(g * CORES + c), cols_sem.at[g * CORES + c], (partner, v))
    own_cols.wait()
    own_rows.wait()
    own_pairs.wait()
    for xx in others_x:
        slab_mask(xx)
        columns = pl.ds(pl.multiple_of(xx * q_own, q_own), q_own)
        slot = xx
        for k in range(CHUNKS):
            at = pl.ds(k * step_rows, step_rows)
            mine[slot, at, :] = jnp.dot(
                rows_all[at, :], slab_masked[:, columns], preferred_element_type=jnp.float32
            )
            send(
                mine.at[slot, at, :], theirs.at[x, at, :], part_sem.at[x, k], (o, z * width + xx)
            )
    slab_share(x)
    for g in range(groups):
        landed(pairs_piece(g * CORES + 1 - c), cols_sem.at[g * CORES + 1 - c])

    @pl.loop(0, CHUNKS)
    def _(k):
        at = pl.ds(pl.multiple_of(k * step_rows, step_rows), step_rows)
        acc[at, :] = jnp.dot(hole_masked[at, :], cols_all[...], preferred_element_type=jnp.float32)

    slab_pass(x)
    slab_mask(x)
    columns = pl.ds(pl.multiple_of(x * q_own, q_own), q_own)

    @pl.loop(0, CHUNKS)
    def _(k):
        at = pl.ds(pl.multiple_of(k * step_rows, step_rows), step_rows)
        acc[at, :] += jnp.dot(
            rows_all[at, :], slab_masked[:, columns], preferred_element_type=jnp.float32
        )

    for k in range(CHUNKS):
        at = pl.ds(k * step_rows, step_rows)
        total = acc[at, :]
        for xx in others_x:
            landed(theirs.at[xx, at, :], part_sem.at[xx, k])
            total = total + theirs[xx, at, :]
        out[:, at] = total.T / (vir_e[...] - occ_e[:, at])

    for copy, when in sent:
        if when is None:
            copy.wait_send()
        else:
            pl.when(when)(copy.wait_send)


def per_device(
    occ_size, vir_size, amplitudes, hole_integrals, particle_integrals, occ_irrep, vir_irrep, occ_energy, vir_energy
):
    width = 1
    while 4 * width * width <= vir_size:
        width *= 2
    lines, groups = vir_size // width, occ_size // CORES
    p_own, q_own = amplitudes.shape
    p_all = p_own * occ_size
    sends = (
        width * (lines - 1) * (2 * groups)
        + 2 * CHUNKS * (lines - 1)
        + 2 * groups - 1
        + (width - 1) * CHUNKS
    )
    vmem = pl.BlockSpec(memory_space=pltpu.VMEM)
    smem = pl.BlockSpec(memory_space=pltpu.SMEM)
    return pl.pallas_call(
        functools.partial(kernel, lines, width, groups),
        out_shape=jax.ShapeDtypeStruct((q_own, p_own), jnp.float32),
        in_specs=[vmem, vmem, pl.BlockSpec(memory_space=pl.ANY), smem, smem, vmem, vmem, vmem, vmem],
        out_specs=vmem,
        scratch_shapes=[
            pltpu.VMEM((lines * q_own, width * q_own), jnp.bfloat16),
            pltpu.VMEM((lines * q_own, width * q_own), jnp.bfloat16),
            pltpu.VMEM((p_own, lines * q_own), jnp.bfloat16),
            pltpu.VMEM((p_all, q_own), jnp.bfloat16),
            pltpu.VMEM((p_own, p_all), jnp.bfloat16),
            pltpu.VMEM((width, p_own, q_own), jnp.float32),
            pltpu.VMEM((width, p_own, q_own), jnp.float32),
            pltpu.VMEM((p_own, q_own), jnp.float32),
            pltpu.SemaphoreType.DMA((sends,)),
            pltpu.SemaphoreType.DMA((lines, occ_size, width)),
            pltpu.SemaphoreType.DMA((lines, CHUNKS)),
            pltpu.SemaphoreType.DMA((occ_size,)),
            pltpu.SemaphoreType.DMA((width, CHUNKS)),
            pltpu.SemaphoreType.DMA((3,)),
        ],
        compiler_params=pltpu.CompilerParams(
            collective_id=0, has_side_effects=True, vmem_limit_bytes=60 * 1024 * 1024
        ),
    )(
        amplitudes, hole_integrals, particle_integrals, occ_irrep, vir_irrep,
        jnp.repeat(occ_irrep, TILE)[None, :], jnp.repeat(vir_irrep, TILE)[None, :],
        occ_energy[None, :], vir_energy[:, None],
    )


def solution(mesh):
    placed = (P("occ", "vir"), P("occ", None), P("vir", None), P(), P(), P("occ"), P("vir"))
    return jax.shard_map(
        functools.partial(per_device, mesh.shape["occ"], mesh.shape["vir"]),
        mesh=mesh, in_specs=placed, out_specs=P("vir", "occ"), check_vma=False,
    )
```

time: 180 us -> 90.3 us (0.50)
  waiting for transfers between devices: 151 us -> 0 us
  Pallas kernels: 0 us -> 83.4 us
  between operations: 14.9 us -> 0.01 us
  matrix products: 11.2 us -> 0 us
  local copies, waits for them, and re-layouts: 3.02 us -> 6.62 us
    reduce_scatter x1 -> x0, waiting for transfers between devices: 133 us -> none  [per_device(): lax.psum_scatter(lax.dot_general(slab_masked, amplitudes, contract_first,...]
    pallas_call x0 -> x1, Pallas kernels: none -> 83.4 us  [per_device(): pl.pallas_call(functools.partial(kernel, lines, width, groups), out_shape...]
    all_gather x1 -> x0, waiting for transfers between devices: 17.1 us -> none  [per_device(): lax.all_gather(amplitudes, 'occ', axis=0, tiled=True)]
    dot_general x2 -> x0, matrix products: 11.2 us -> none  [the longest x1 8.08 us: per_device(): lax.dot_general(slab_masked, amplitudes, contract_first, preferred_elemen...]
    broadcast_in_dim x2 -> x3, local copies, waits for them, and re-layouts: 0.8 us -> 2.98 us  [the longest x1 1.53 us: per_device(): vir_energy[:, None]]
  transfers between devices with their start and end apart: 2 -> 0, of which waited for: 2 -> 0; matrix products, arithmetic and copies ran while one was open for 5% -> 0% of each run, Pallas kernels for 0% -> 0%
where the time goes in v1:
time: 90.3 us; the launch traced here: 90.1 us
  Pallas kernels  83.4 us (92%)
  local copies, waits for them, and re-layouts  6.62 us (7%)
    pallas_call x1, Pallas kernels, per_device(): pl.pallas_call(functools.partial(kernel, lines, width, groups), out_shape...  83.4 us
    unnamed x1, local copies, waits for them, and re-layouts  2.26 us

profile of v1, /device:TPU:0, one launch (start us, length us, event | category | flops | bytes accessed | tf_op | source)
XLA Modules:
  0.0 90.1 jit_solution(3814783149450031719)
XLA Ops:
  0.0 0.7 broadcast_in_dim.12
  0.7 0.7 broadcast_in_dim_reshape.6.occ_labels
  1.4 0.7 broadcast_in_dim.13
  2.1 0.7 broadcast_in_dim_reshape.7.vir_labels
  2.8 1.5 %copy.8.vir_e = f32[512,1]{1,0:T(8,128)} copy(f32[512,1]{0,1:T(1,128)} %bitcast.2) | data formatting | bytes 4096 | tf_op jit(solution)/shard_map/broadcast_in_dim | solution.py:263
  4.4 83.4 %shard_map.73 = f32[512,512]{1,0:T(8,128)} custom-call(bf16[512,512]{1,0:T(8,128)(2,1)} %amp.1, bf16[512,2048]{1,0:T(8,128)(2,1)} %hole.1, bf16[512,4096]{1,0:T(8,128)(2,1)} %slab.1, s32[32]{0:T(128)} %occ_irrep.1, s32[64]{0:T(128)} %vir_irrep.1, s32[1,2048]{1,0:T(1,128)} %broadcast_in_dim_reshape.6.occ_labels, ...), custom_call_target="tpu_custom_call" | custom-call | tf_op jit(solution)/shard_map/pallas_call | solution.py:236
  87.8 2.3 %copy.10 = f32[512,512]{1,0:T(8,128)} copy(f32[512,512]{1,0:T(8,128)} %shard_map.73) | data formatting | bytes 2097152

commit v2 on v1

--- a/solution.py
+++ b/solution.py
@@ -14,7 +14,8 @@
 
 
 def kernel(
-    lines, width, groups, amp, hole, slab, occ_irrep, vir_irrep, occ_labels, vir_labels, occ_e, vir_e, out,
+    lines, width, groups, amp, hole, slab, occ_irrep, vir_irrep, occ_e, vir_e, out,
+    occ_labels, vir_labels,
     slab_all, slab_masked, rows_all, cols_all, hole_masked, mine, theirs, acc,
     send_sem, slab_sem, rows_sem, cols_sem, part_sem, local_sem,
 ):
@@ -124,8 +125,8 @@
         send(src, rows_piece(z, k), rows_sem.at[z, k], up, has_up)
         send(src, rows_piece(z, k), rows_sem.at[z, k], down, has_down)
 
-    def rows_relay(k):
-        for d in range(1, lines):
+    def rows_relay(k, distances):
+        for d in distances:
             for zz, there, onward, device in (
                 (z - d, z - d >= 0, has_up, up), (z + d, z + d < lines, has_down, down),
             ):
@@ -147,6 +148,15 @@
 
     tiles = p_own // TILE
 
+    half = lax.broadcasted_iota(jnp.int32, (1, 2 * TILE), 1) < TILE
+    for labels, irreps in ((occ_labels, occ_irrep), (vir_labels, vir_irrep)):
+
+        @pl.loop(0, irreps.shape[0] // 2)
+        def _(i):
+            labels[:, pl.ds(pl.multiple_of(i * 2 * TILE, 2 * TILE), 2 * TILE)] = jnp.where(
+                half, irreps[2 * i], irreps[2 * i + 1]
+            )
+
     @pl.loop(0, tiles)
     def _(i):
         at = pl.ds(pl.multiple_of(i * TILE, TILE), TILE)
@@ -157,12 +167,11 @@
 
     for xx in others_x:
         slab_share(xx)
-    rows_relay(0)
+    for k in range(CHUNKS):
+        rows_relay(k, range(1, 2))
+    slab_send(x)
     for xx in others_x:
         slab_pass(xx)
-    for k in range(1, CHUNKS):
-        rows_relay(k)
-    slab_send(x)
     for g in others_h:
         landed(pairs_piece(g * CORES + c), cols_sem.at[g * CORES + c])
         send(pairs_piece(g * CORES + c), pairs_piece(g * CORES + c), cols_sem.at[g * CORES + c], (partner, v))
@@ -171,15 +180,16 @@
     own_pairs.wait()
     for xx in others_x:
         slab_mask(xx)
-        columns = pl.ds(pl.multiple_of(xx * q_own, q_own), q_own)
-        slot = xx
-        for k in range(CHUNKS):
-            at = pl.ds(k * step_rows, step_rows)
-            mine[slot, at, :] = jnp.dot(
+    for k in range(CHUNKS):
+        rows_relay(k, range(2, lines))
+        at = pl.ds(k * step_rows, step_rows)
+        for xx in others_x:
+            columns = pl.ds(pl.multiple_of(xx * q_own, q_own), q_own)
+            mine[xx, at, :] = jnp.dot(
                 rows_all[at, :], slab_masked[:, columns], preferred_element_type=jnp.float32
             )
             send(
-                mine.at[slot, at, :], theirs.at[x, at, :], part_sem.at[x, k], (o, z * width + xx)
+                mine.at[xx, at, :], theirs.at[x, at, :], part_sem.at[x, k], (o, z * width + xx)
             )
     slab_share(x)
     for g in range(groups):
@@ -201,13 +211,14 @@
             rows_all[at, :], slab_masked[:, columns], preferred_element_type=jnp.float32
         )
 
+    vir_column = jnp.broadcast_to(vir_e[...], (step_rows, q_own)).T
     for k in range(CHUNKS):
         at = pl.ds(k * step_rows, step_rows)
         total = acc[at, :]
         for xx in others_x:
             landed(theirs.at[xx, at, :], part_sem.at[xx, k])
             total = total + theirs[xx, at, :]
-        out[:, at] = total.T / (vir_e[...] - occ_e[:, at])
+        out[:, at] = total.T / (vir_column - occ_e[:, at])
 
     for copy, when in sent:
         if when is None:
@@ -236,9 +247,11 @@
     return pl.pallas_call(
         functools.partial(kernel, lines, width, groups),
         out_shape=jax.ShapeDtypeStruct((q_own, p_own), jnp.float32),
-        in_specs=[vmem, vmem, pl.BlockSpec(memory_space=pl.ANY), smem, smem, vmem, vmem, vmem, vmem],
+        in_specs=[vmem, vmem, pl.BlockSpec(memory_space=pl.ANY), smem, smem, vmem, vmem],
         out_specs=vmem,
         scratch_shapes=[
+            pltpu.VMEM((1, occ_irrep.shape[0] * TILE), jnp.int32),
+            pltpu.VMEM((1, vir_irrep.shape[0] * TILE), jnp.int32),
             pltpu.VMEM((lines * q_own, width * q_own), jnp.bfloat16),
             pltpu.VMEM((lines * q_own, width * q_own), jnp.bfloat16),
             pltpu.VMEM((p_own, lines * q_own), jnp.bfloat16),
@@ -259,8 +272,7 @@
         ),
     )(
         amplitudes, hole_integrals, particle_integrals, occ_irrep, vir_irrep,
-        jnp.repeat(occ_irrep, TILE)[None, :], jnp.repeat(vir_irrep, TILE)[None, :],
-        occ_energy[None, :], vir_energy[:, None],
+        occ_energy[None, :], vir_energy[None, :],
     )
 
 

time: 90.3 us -> 78.4 us (0.87)
  Pallas kernels: 83.4 us -> 75.4 us
  local copies, waits for them, and re-layouts: 6.62 us -> 2.26 us
    pallas_call x1, Pallas kernels: 83.4 us -> 75.4 us  [per_device(): pl.pallas_call(functools.partial(kernel, lines, width, groups), out_shape...]
    broadcast_in_dim x3 -> x0, local copies, waits for them, and re-layouts: 2.98 us -> none  [the longest x1 1.53 us: per_device(): vir_energy[:, None]]
    another operation x2 -> x0, local copies, waits for them, and re-layouts: 1.37 us -> none  [the longest x1 0.69 us: per_device(): jnp.repeat(vir_irrep, TILE)[None, :]]
where the time goes in v2:
time: 78.4 us; the launch traced here: 77.6 us
  Pallas kernels  75.4 us (96%)
  local copies, waits for them, and re-layouts  2.26 us (3%)
    pallas_call x1, Pallas kernels, per_device(): pl.pallas_call(functools.partial(kernel, lines, width, groups), out_shape...  75.4 us
    unnamed x1, local copies, waits for them, and re-layouts  2.26 us

profile of v2, /device:TPU:0, one launch (start us, length us, event | category | flops | bytes accessed | tf_op | source)
XLA Modules:
  0.0 77.6 jit_solution(10256918091839971250)
XLA Ops:
  0.0 75.4 %shard_map.73 = f32[512,512]{1,0:T(8,128)} custom-call(bf16[512,512]{1,0:T(8,128)(2,1)} %amp.1, bf16[512,2048]{1,0:T(8,128)(2,1)} %hole.1, bf16[512,4096]{1,0:T(8,128)(2,1)} %slab.1, s32[32]{0:T(128)} %occ_irrep.1, s32[64]{0:T(128)} %vir_irrep.1, f32[1,512]{1,0:T(1,128)} %bitcast.2, f32[1,512]{1,0:T(1,128)} %bitcast.3), custom_call_target="tpu_custom_call" | custom-call | tf_op jit(solution)/shard_map/pallas_call | solution.py:247
  75.4 2.3 %copy.9 = f32[512,512]{1,0:T(8,128)} copy(f32[512,512]{1,0:T(8,128)} %shard_map.73) | data formatting | bytes 2097152
